TPU v7x, 32 devices: a whole 2x2x4 slice. The times are simulated.
32 devices in a mesh: site: 8 (over z, x), dom: 4 (over y, core).
Axes of the slice: x: 2, y: 2, z: 4, core: 2. Of those that a mesh axis runs over, the one named last changes fastest.
Arguments:
- top_partial: float32 [16, 61, 4, 8192], P(None, None, 'dom', 'site'), may hold values from 0.001 to 1
- bottom_partial: float32 [16, 61, 4, 8192], P(None, None, 'dom', 'site'), may hold values from 0.001 to 1
- left_vectors: float32 [256, 61, 61], P('dom'), may hold values from 0.05 to 1
- right_vectors: float32 [256, 61, 61], P('dom'), may hold values from 0.05 to 1
- decay_rates: float32 [256, 61], P('dom'), may hold values from 0.05 to 8
- state_weights: float32 [256, 61], P('dom'), may hold values from 0.002 to 0.05
- part_rates: float32 [256], P('dom'), may hold values from 0.3 to 3
- branch_lengths: float32 [1997], replicated, may hold values from 0.02 to 0.5
- pattern_weights: int32 [4, 8192], P('dom', 'site'), may hold values from 0 to 9
- block_partition: int32 [4, 64], P('dom', 'site'), may hold values from 0 to 255
- chosen_branches: int32 [16], replicated, may hold values from 0 to 1996, as said below
Outputs:
- site_loglik: float32 [16, 4, 8192], P(None, 'dom', 'site')
- part_derivs: float32 [2, 16, 256], P(None, None, 'dom')
- new_lengths: float32 [1997], replicated
Inputs may be any that keep to these rules, and one draw needn't show every extreme that they name: `chosen_branches`: distinct branch numbers.
All inputs are finite; a program needn't handle non-finite values.
Results may differ from a plain program's by a relative error of at most 0.0003.
Values sent between devices are 32-bit elements; how exact they have to be, the bound alone decides.
A program may use at most 64 MiB of HBM per device.

v0:
```python
import jax
import jax.numpy as jnp
from jax import lax
from jax.sharding import PartitionSpec as P

BLK = 128


def project(upper, lower, vec_left, vec_right, state_w):
    scaled = upper * jnp.transpose(state_w)[None, :, :, None]
    lefts = jnp.einsum("binl,nik->bknl", scaled, vec_left, precision=lax.Precision.HIGHEST)
    rights = jnp.einsum("nkj,bjnl->bknl", vec_right, lower, precision=lax.Precision.HIGHEST)
    return (lefts, rights)


def finish(lefts, rights, exponent, times, weight_f):
    joint = lefts * rights
    expo = jnp.transpose(exponent)[None, :, :, None]
    decayed = joint * jnp.exp(expo * times[:, None, None, None])
    like_zero = jnp.sum(decayed, axis=1)
    like_one = jnp.sum(decayed * expo, axis=1)
    like_two = jnp.sum(decayed * expo * expo, axis=1)
    first = like_one / like_zero
    second = like_two / like_zero - first * first
    loglik = weight_f[None] * jnp.log(like_zero)
    sums = jnp.stack(
        [jnp.sum(weight_f[None] * first, axis=-1), jnp.sum(weight_f[None] * second, axis=-1)]
    )
    return (loglik, sums)


def on_device(
    top_partial,
    bottom_partial,
    left_vectors,
    right_vectors,
    decay_rates,
    state_weights,
    part_rates,
    branch_lengths,
    pattern_weights,
    block_partition,
    chosen_branches,
):
    times = branch_lengths[chosen_branches]
    branches = top_partial.shape[0]
    states = top_partial.shape[1]
    sites_here = top_partial.shape[3]
    nblocks = sites_here // BLK
    upper = top_partial.reshape(branches, states, nblocks, BLK)
    lower = bottom_partial.reshape(branches, states, nblocks, BLK)
    blocks = block_partition[0]
    owned = left_vectors.shape[0]
    groups = lax.axis_size("dom")
    parts_all = owned * groups
    wanted = lax.all_gather(block_partition, "dom", axis=0, tiled=True)
    relative = wanted - lax.axis_index("dom") * owned
    inside = jnp.logical_and(relative >= 0, relative < owned).astype(jnp.float32)
    clipped = jnp.clip(relative, 0, owned - 1)
    send_left = left_vectors[clipped] * inside[:, :, None, None]
    send_right = right_vectors[clipped] * inside[:, :, None, None]
    send_decay = decay_rates[clipped] * inside[:, :, None]
    send_weight = state_weights[clipped] * inside[:, :, None]
    send_rate = part_rates[clipped] * inside
    received = (
        lax.all_to_all(send_left, "dom", split_axis=0, concat_axis=0, tiled=True),
        lax.all_to_all(send_right, "dom", split_axis=0, concat_axis=0, tiled=True),
        lax.all_to_all(send_decay, "dom", split_axis=0, concat_axis=0, tiled=True),
        lax.all_to_all(send_weight, "dom", split_axis=0, concat_axis=0, tiled=True),
        lax.all_to_all(send_rate, "dom", split_axis=0, concat_axis=0, tiled=True),
    )
    vec_left = jnp.sum(received[0], axis=0)
    vec_right = jnp.sum(received[1], axis=0)
    decay_b = jnp.sum(received[2], axis=0)
    weight_b = jnp.sum(received[3], axis=0)
    rate_b = jnp.sum(received[4], axis=0)
    exponent = -decay_b * rate_b[:, None]
    lefts, rights = project(upper, lower, vec_left, vec_right, weight_b)
    weight_f = pattern_weights[0].astype(jnp.float32).reshape(nblocks, BLK)
    loglik, sums = finish(lefts, rights, exponent, times, weight_f)
    onehot = (blocks[:, None] == jnp.arange(parts_all, dtype=jnp.int32)[None, :]).astype(
        jnp.float32
    )
    part_local = jnp.einsum("abn,np->abp", sums, onehot, precision=lax.Precision.HIGHEST)
    everything = lax.psum(part_local, ("site", "dom"))
    share = lax.dynamic_slice_in_dim(everything, lax.axis_index("dom") * owned, owned, 2)
    totals = jnp.sum(everything, axis=2)
    updated = times - totals[0] / totals[1]
    new_lengths = branch_lengths.at[chosen_branches].set(updated)
    return (loglik.reshape(branches, 1, sites_here), share, new_lengths)


def solution(mesh):
    return jax.shard_map(
        on_device,
        mesh=mesh,
        in_specs=(
            P(None, None, "dom", "site"),
            P(None, None, "dom", "site"),
            P("dom", None, None),
            P("dom", None, None),
            P("dom", None),
            P("dom", None),
            P("dom"),
            P(),
            P("dom", "site"),
            P("dom", "site"),
            P(),
        ),
        out_specs=(P(None, "dom", "site"), P(None, None, "dom"), P()),
        check_vma=False,
    )
```

profile of v0, /device:TPU:0, one launch (start us, length us, event | category | flops | bytes accessed | tf_op | source)
XLA Modules:
  0.0 121.8 jit_solution(4191838396032848199)
XLA Ops:
  0.6 0.8 copy.76
  1.5 6.2 %all-gather = s32[4,1,8]{2,1,0:T(1,128)S(1)} all-gather(s32[1,1,8]{2,1,0:T(1,128)} %bitcast.55), channel_id=1, replica_groups=mesh['site'=8,'dom'=4] {'dom'}, dimensions={0}, use_global_device_ids=true | all-gather | bytes 160 | tf_op jit(solution)/shard_map/all_gather | solution.py:56
  7.8 1.4 %gather_fusion.4 = f32[32]{0:T(128)S(1)} fusion(f32[64]{0:T(128)} %param.17, s32[1024]{0:T(1024)S(1)} %pad_clamp_fusion.1), kind=kCustom, calls=%fused_computation.4 | custom fusion | bytes 384 | tf_op jit(solution)/shard_map/gather | solution.py:64
  9.9 3.2 %all-to-all-start.4 = ((f32[4,1,8]{2,1,0:T(1,128)}), f32[4,1,8]{2,1,0:T(1,128)S(1)}, u32[]{:S(2)}, u32[]{:S(2)}) async-start(f32[4,1,8]{2,1,0:T(1,128)} %bitcast.14), calls=%async_computation.4 | async-start | bytes 4096 | tf_op jit(solution)/shard_map/all_to_all | solution.py:70
  13.1 1.3 %gather_fusion.3 = f32[32,61]{1,0:T(8,128)S(1)} fusion(f32[64,61]{1,0:T(8,128)} %param.15, s32[1024]{0:T(1024)S(1)} %pad_clamp_fusion.1), kind=kCustom, calls=%fused_computation.3 | custom fusion | bytes 15744 | tf_op jit(solution)/shard_map/gather | solution.py:62
  14.4 1.3 %gather_fusion.1 = f32[32,61]{1,0:T(8,128)S(1)} fusion(f32[64,61]{1,0:T(8,128)} %param.16, s32[1024]{0:T(1024)S(1)} %pad_clamp_fusion.1), kind=kCustom, calls=%fused_computation.1 | custom fusion | bytes 15744 | tf_op jit(solution)/shard_map/gather | solution.py:63
  16.8 3.2 %all-to-all-start.3 = ((f32[4,1,488]{2,1,0:T(1,128)}), f32[4,1,488]{2,1,0:T(1,128)S(1)}, u32[]{:S(2)}, u32[]{:S(2)}) async-start(f32[4,1,488]{2,1,0:T(1,128)} %reshape.156), calls=%async_computation.3 | async-start | bytes 16384 | tf_op jit(solution)/shard_map/all_to_all | solution.py:68
  20.7 2.7 %gather_fusion.2 = f32[32,61,61]{2,0,1:T(8,128)S(1)} fusion(f32[64,61,61]{2,0,1:T(8,128)S(1)} %copy-done, s32[1024]{0:T(1024)S(1)} %pad_clamp_fusion.1), kind=kCustom, calls=%fused_computation.2 | custom fusion | bytes 952704 | tf_op jit(solution)/shard_map/gather | solution.py:61
  23.5 5.3 %gather_fusion = f32[32,61,61]{2,0,1:T(8,128)} fusion(f32[64,61,61]{2,0,1:T(8,128)} %param.13, s32[1024]{0:T(1024)S(1)} %pad_clamp_fusion.1), kind=kCustom, calls=%fused_computation | custom fusion | bytes 952704 | tf_op jit(solution)/shard_map/gather | solution.py:60
  28.8 3.4 %all-to-all-start.1 = ((f32[4,1,488]{2,1,0:T(1,128)}), f32[4,1,488]{2,1,0:T(1,128)S(1)}, u32[]{:S(2)}, u32[]{:S(2)}) async-start(f32[4,1,488]{2,1,0:T(1,128)} %reshape.158), calls=%async_computation.1 | async-start | bytes 16384 | tf_op jit(solution)/shard_map/all_to_all | solution.py:69
  32.2 2.8 %copy_multiply_fusion.5 = (f32[4,8,61,61]{3,1,2,0:T(8,128)}, f32[4,8,61,61]{3,1,2,0:T(8,128)}) fusion(f32[4,8]{1,0:T(4,128)S(1)} %bitcast_convert_fusion, f32[32,61,61]{2,0,1:T(8,128)S(1)} %gather_fusion.2, f32[32,61,61]{2,0,1:T(8,128)} %gather_fusion), kind=kLoop, calls=%fused_computation.16 | loop fusion | flops 238144 | bytes 1905280 | tf_op jit(solution)/shard_map/mul | solution.py:60
  35.0 3.2 %reshape.160 = f32[4,1,29768]{2,1,0:T(1,128)} reshape(f32[4,61,8,61]{3,2,1,0:T(8,128)} %bitcast.46) | data formatting | bytes 952576
  38.2 3.5 %all-to-all-start = ((f32[4,1,29768]{2,1,0:T(1,128)}), f32[4,1,29768]{2,1,0:T(1,128)S(1)}, u32[]{:S(2)}, u32[]{:S(2)}) async-start(f32[4,1,29768]{2,1,0:T(1,128)} %reshape.160), calls=%async_computation | async-start | bytes 954368 | tf_op jit(solution)/shard_map/all_to_all | solution.py:66
  41.7 3.1 %reshape.154 = f32[4,1,29768]{2,1,0:T(1,128)} reshape(f32[4,61,8,61]{3,2,1,0:T(8,128)} %bitcast.45) | data formatting | bytes 952576
  48.3 1.7 %all-to-all-done = f32[4,1,29768]{2,1,0:T(1,128)S(1)} async-done(((f32[4,1,29768]{2,1,0:T(1,128)}), f32[4,1,29768]{2,1,0:T(1,128)S(1)}, u32[]{:S(2)}, u32[]{:S(2)}) %all-to-all-start) | async-done | bytes 476320 | tf_op jit(solution)/shard_map/all_to_all | solution.py:66
  49.9 4.3 %all-to-all-start.2 = ((f32[4,1,29768]{2,1,0:T(1,128)}), f32[4,1,29768]{2,1,0:T(1,128)}, u32[]{:S(2)}, u32[]{:S(2)}) async-start(f32[4,1,29768]{2,1,0:T(1,128)} %reshape.154), calls=%async_computation.2 | async-start | bytes 954368 | tf_op jit(solution)/shard_map/all_to_all | solution.py:67
  54.3 2.1 %reduce.4 = f32[4,29768]{1,0:T(4,128)S(1)} reduce(f32[4,1,29768]{2,1,0:T(1,128)S(1)} %all-to-all-done, f32[]{:T(128)} %broadcast.86), dimensions={1}, to_apply=%all_to_all.18.reduce_sub_computation | reduce | bytes 952580 | tf_op jit(solution)/shard_map/all_to_all | solution.py:66
  57.0 0.8 bitcast_reduce_fusion
  57.7 4.7 %all-to-all-done.2 = f32[4,1,29768]{2,1,0:T(1,128)} async-done(((f32[4,1,29768]{2,1,0:T(1,128)}), f32[4,1,29768]{2,1,0:T(1,128)}, u32[]{:S(2)}, u32[]{:S(2)}) %all-to-all-start.2) | async-done | bytes 476320 | tf_op jit(solution)/shard_map/all_to_all | solution.py:67
  62.4 2.9 %reduce.2 = f32[4,29768]{1,0:T(4,128)S(1)} reduce(f32[4,1,29768]{2,1,0:T(1,128)} %all-to-all-done.2, f32[]{:T(128)} %broadcast.86), dimensions={1}, to_apply=%all_to_all.20.reduce_sub_computation | reduce | bytes 952580 | tf_op jit(solution)/shard_map/all_to_all | solution.py:67
  66.0 6.8 %fusion = f32[8,61,16,128]{3,1,2,0:T(8,128)S(1)} fusion(f32[16,61,8,128]{3,2,1,0:T(8,128)} %bitcast.44, f32[8,61,61,1]{2,0,1,3:T(8,128)S(1)} %bitcast.47), kind=kOutput, calls=%fused_computation.8 | convolution fusion | flops 731578368 | bytes 8114464 | tf_op jit(solution)/shard_map/nkj,bjnl->bknl/dot_general | solution.py:12
  72.9 6.4 %multiply_reduce_fusion.1 = (f32[16,8,128]{2,0,1:T(8,128)S(1)}, f32[16,8,128]{2,0,1:T(8,128)S(1)}, f32[16,8,128]{2,0,1:T(8,128)S(1)}) fusion(f32[61,8]{0,1:T(8,128)S(1)} %copy-done.4, f32[16,61,8]{1,0,2:T(8,128)S(1)} %multiply_exponential_fusion, f32[8,61,16,128]{3,1,2,0:T(8,128)S(1)} %fusion, f32[16,61,8,128]{3,2,1,0:T(8,128)S(1)} %bitcast.57, ...), kind=kOutput, calls=%fused_computation.13 | convolution fusion | flops 739524608 | bytes 8346208 | tf_op jit(solution)/shard_map/binl,nik->bknl/dot_general | solution.py:11
  79.7 39.9 %psum.7 = f32[2,16,256]{2,1,0:T(8,128)S(1)} all-reduce(f32[2,16,256]{2,1,0:T(8,128)S(1)} %fusion.6), channel_id=1, replica_groups=mesh['site'=8,'dom'=4] {'site','dom'}, use_global_device_ids=true, to_apply=%region_10.11 | all-reduce | flops 8192 | bytes 65536 | tf_op jit(solution)/shard_map/psum | solution.py:85
  121.1 0.7 copy.45
  (68 shorter events, 9.1 us)
Async XLA Ops:
  0.6 20.1 %copy-start = (f32[64,61,61]{2,0,1:T(8,128)S(1)}, f32[64,61,61]{2,0,1:T(8,128)}, u32[]{:S(2)}) copy-start(f32[64,61,61]{2,0,1:T(8,128)} %param.14) | copy-start | bytes 2857732
  9.9 6.9 %all-to-all-start.4 = ((f32[4,1,8]{2,1,0:T(1,128)}), f32[4,1,8]{2,1,0:T(1,128)S(1)}, u32[]{:S(2)}, u32[]{:S(2)}) async-start(f32[4,1,8]{2,1,0:T(1,128)} %bitcast.14), calls=%async_computation.4 | async-start | bytes 4096 | tf_op jit(solution)/shard_map/all_to_all | solution.py:70
  16.8 12.0 %all-to-all-start.3 = ((f32[4,1,488]{2,1,0:T(1,128)}), f32[4,1,488]{2,1,0:T(1,128)S(1)}, u32[]{:S(2)}, u32[]{:S(2)}) async-start(f32[4,1,488]{2,1,0:T(1,128)} %reshape.156), calls=%async_computation.3 | async-start | bytes 16384 | tf_op jit(solution)/shard_map/all_to_all | solution.py:68
  28.8 12.9 %copy-start.13 = (s32[16]{0:T(128)S(1)}, s32[16]{0:T(128)}, u32[]{:S(2)}) copy-start(s32[16]{0:T(128)} %param.21) | copy-start | bytes 196
  28.8 12.9 %copy-start.7 = (s32[1,1024]{1,0:T(1,128)S(1)}, s32[1,1024]{1,0:T(1,128)}, u32[]{:S(2)}) copy-start(s32[1,1024]{1,0:T(1,128)} %param.19) | copy-start | bytes 12292
  28.8 9.4 %all-to-all-start.1 = ((f32[4,1,488]{2,1,0:T(1,128)}), f32[4,1,488]{2,1,0:T(1,128)S(1)}, u32[]{:S(2)}, u32[]{:S(2)}) async-start(f32[4,1,488]{2,1,0:T(1,128)} %reshape.158), calls=%async_computation.1 | async-start | bytes 16384 | tf_op jit(solution)/shard_map/all_to_all | solution.py:69
  38.2 11.8 %all-to-all-start = ((f32[4,1,29768]{2,1,0:T(1,128)}), f32[4,1,29768]{2,1,0:T(1,128)S(1)}, u32[]{:S(2)}, u32[]{:S(2)}) async-start(f32[4,1,29768]{2,1,0:T(1,128)} %reshape.160), calls=%async_computation | async-start | bytes 954368 | tf_op jit(solution)/shard_map/all_to_all | solution.py:66
  41.7 3.2 %copy-start.9 = (s32[16]{0:T(128)}, s32[16]{0:T(128)S(1)}, u32[]{:S(2)}) copy-start(s32[16]{0:T(128)S(1)} %compare_select_fusion.1) | copy-start | bytes 196
  45.5 8.7 %copy-start.5 = (f32[16]{0:T(128)}, f32[16]{0:T(128)S(1)}, u32[]{:S(2)}) copy-start(f32[16]{0:T(128)S(1)} %gather_fusion.5) | copy-start | bytes 196
  48.2 6.1 %copy-start.3 = (f32[61,8]{0,1:T(8,128)}, f32[61,8]{0,1:T(8,128)S(1)}, u32[]{:S(2)}) copy-start(f32[61,8]{0,1:T(8,128)S(1)} %multiply_bitcast_fusion) | copy-start | bytes 5860
  49.9 12.5 %all-to-all-start.2 = ((f32[4,1,29768]{2,1,0:T(1,128)}), f32[4,1,29768]{2,1,0:T(1,128)}, u32[]{:S(2)}, u32[]{:S(2)}) async-start(f32[4,1,29768]{2,1,0:T(1,128)} %reshape.154), calls=%async_computation.2 | async-start | bytes 954368 | tf_op jit(solution)/shard_map/all_to_all | solution.py:67
  66.0 6.9 %copy-start.2 = (f32[8,61,61]{2,0,1:T(8,128)S(1)}, f32[8,61,61]{2,0,1:T(8,128)}, u32[]{:S(2)}) copy-start(f32[8,61,61]{2,0,1:T(8,128)} %bitcast_reduce_fusion) | copy-start | bytes 357220
  66.0 6.9 %copy-start.4 = (f32[61,8]{0,1:T(8,128)S(1)}, f32[61,8]{0,1:T(8,128)}, u32[]{:S(2)}) copy-start(f32[61,8]{0,1:T(8,128)} %copy-done.3) | copy-start | bytes 5860
  66.0 6.9 %copy-start.8 = (f32[8,61]{1,0:T(8,128)S(1)}, f32[8,61]{1,0:T(8,128)}, u32[]{:S(2)}) copy-start(f32[8,61]{1,0:T(8,128)} %reduce_sum.100) | copy-start | bytes 5860
  66.0 6.9 %copy-start.12 = (f32[16,61,1,1024]{3,2,1,0:T(1,128)S(1)}, f32[16,61,1,1024]{3,2,1,0:T(1,128)}, u32[]{:S(2)}) copy-start(f32[16,61,1,1024]{3,2,1,0:T(1,128)} %param.11) | copy-start | bytes 11993092
  72.9 6.6 %copy-start.11 = (s32[1,8]{1,0:T(1,128)S(1)}, s32[1,8]{1,0:T(1,128)}, u32[]{:S(2)}) copy-start(s32[1,8]{1,0:T(1,128)} %param.20) | copy-start | bytes 100
  72.9 47.5 %copy-start.6 = (f32[16]{0:T(128)S(1)}, f32[16]{0:T(128)}, u32[]{:S(2)}) copy-start(f32[16]{0:T(128)} %copy-done.5) | copy-start | bytes 196
  72.9 47.5 %copy-start.10 = (s32[16]{0:T(128)S(1)}, s32[16]{0:T(128)}, u32[]{:S(2)}) copy-start(s32[16]{0:T(128)} %copy-done.9) | copy-start | bytes 196
  121.0 0.8 copy-start.1
where the time goes:
time: 123 us; the launch traced here: 122 us
  blocking collectives  46.1 us (37%)
  local copies, waits for them, and re-layouts  25.3 us (21%)
  starting transfers between devices  17.6 us (14%)
  matrix products  13.5 us (11%)
  other arithmetic  11.7 us (10%)
  waiting for transfers between devices  6.6 us (5%)
    psum x1, blocking collectives, on_device(): everything = lax.psum(part_local, ('site', 'dom'))  39.9 us
    unnamed x38, local copies, waits for them, and re-layouts  10.6 us
    dot_general x1, matrix products, project(): jnp.einsum('nkj,bjnl->bknl', vec_right, lower, precision=lax.Precision.HI...  6.82 us
    dot_general x1, matrix products, project(): jnp.einsum('binl,nik->bknl', scaled, vec_left, precision=lax.Precision.HI...  6.42 us
    all_gather x1, blocking collectives, on_device(): wanted = lax.all_gather(block_partition, 'dom', axis=0, tiled=True)  6.22 us
    gather x1, local copies, waits for them, and re-layouts, on_device(): send_left = left_vectors[clipped] * inside[:, :, None, None]  5.29 us
    all_to_all x1, waiting for transfers between devices, on_device(): lax.all_to_all(send_right, 'dom', split_axis=0, concat_axis=0, tiled=True)  4.67 us
    all_to_all x1, starting transfers between devices, on_device(): lax.all_to_all(send_right, 'dom', split_axis=0, concat_axis=0, tiled=True)  4.3 us
  transfers between devices with their start and end apart: 5, of which 3 were waited for; matrix products, arithmetic and copies ran while one was open for 23% of the time, Pallas kernels for 0%

commit v1 on v0

--- a/solution.py
+++ b/solution.py
@@ -82,7 +82,7 @@
         jnp.float32
     )
     part_local = jnp.einsum("abn,np->abp", sums, onehot, precision=lax.Precision.HIGHEST)
-    everything = lax.psum(part_local, ("site", "dom"))
+    everything = jnp.sum(lax.all_gather(part_local, ("site", "dom")), axis=0)
     share = lax.dynamic_slice_in_dim(everything, lax.axis_index("dom") * owned, owned, 2)
     totals = jnp.sum(everything, axis=2)
     updated = times - totals[0] / totals[1]

time: 123 us -> 153 us (1.24)
  waiting for transfers between devices: 6.6 us -> 60.2 us
  blocking collectives: 46.1 us -> 6.22 us
  between operations: 0.99 us -> 14.4 us
  other arithmetic: 11.7 us -> 14.4 us
    all_gather x0 -> x1, waiting for transfers between devices: none -> 53.6 us  [on_device(): everything = jnp.sum(lax.all_gather(part_local, ('site', 'dom')), axis=0)]
    psum x1 -> x0, blocking collectives: 39.9 us -> none  [on_device(): everything = lax.psum(part_local, ('site', 'dom'))]
  transfers between devices with their start and end apart: 5 -> 6, of which waited for: 3 -> 4; matrix products, arithmetic and copies ran while one was open for 23% -> 19% of each run, Pallas kernels for 0% -> 0%
where the time goes in v1:
time: 153 us; the launch traced here: 152 us
  waiting for transfers between devices  60.2 us (39%)
  local copies, waits for them, and re-layouts  25.3 us (17%)
  starting transfers between devices  17.7 us (12%)
  other arithmetic  14.4 us (9%)
  between operations  14.4 us (9%)
  matrix products  14.1 us (9%)
  blocking collectives  6.22 us (4%)
    all_gather x1, waiting for transfers between devices, on_device(): everything = jnp.sum(lax.all_gather(part_local, ('site', 'dom')), axis=0)  53.6 us
    unnamed x38, local copies, waits for them, and re-layouts  10.6 us
    dot_general x1, matrix products, project(): jnp.einsum('nkj,bjnl->bknl', vec_right, lower, precision=lax.Precision.HI...  6.82 us
    dot_general x1, matrix products, project(): jnp.einsum('binl,nik->bknl', scaled, vec_left, precision=lax.Precision.HI...  6.42 us
    all_gather x1, blocking collectives, on_device(): wanted = lax.all_gather(block_partition, 'dom', axis=0, tiled=True)  6.22 us
    gather x1, local copies, waits for them, and re-layouts, on_device(): send_left = left_vectors[clipped] * inside[:, :, None, None]  5.29 us
    all_to_all x1, waiting for transfers between devices, on_device(): lax.all_to_all(send_right, 'dom', split_axis=0, concat_axis=0, tiled=True)  4.62 us
    all_to_all x1, starting transfers between devices, on_device(): lax.all_to_all(send_right, 'dom', split_axis=0, concat_axis=0, tiled=True)  4.12 us
  transfers between devices with their start and end apart: 6, of which 4 were waited for; matrix products, arithmetic and copies ran while one was open for 19% of the time, Pallas kernels for 0%

profile of v1, /device:TPU:0, one launch (start us, length us, event | category | flops | bytes accessed | tf_op | source)
XLA Modules:
  0.0 152.3 jit_solution(3823639845382890914)
XLA Ops:
  7.2 0.8 copy.110
  8.0 6.2 %all-gather.1 = s32[4,1,8]{2,1,0:T(1,128)S(1)} all-gather(s32[1,1,8]{2,1,0:T(1,128)} %bitcast.59), channel_id=1, replica_groups=mesh['site'=8,'dom'=4] {'dom'}, dimensions={0}, use_global_device_ids=true | all-gather | bytes 160 | tf_op jit(solution)/shard_map/all_gather | solution.py:56
  14.4 1.4 gather_fusion.4
  16.4 3.2 %all-to-all-start.4 = ((f32[4,1,8]{2,1,0:T(1,128)}), f32[4,1,8]{2,1,0:T(1,128)S(1)}, u32[]{:S(2)}, u32[]{:S(2)}) async-start(f32[4,1,8]{2,1,0:T(1,128)} %bitcast.14), calls=%async_computation.4 | async-start | bytes 4096 | tf_op jit(solution)/shard_map/all_to_all | solution.py:70
  19.6 1.3 gather_fusion.3
  21.0 1.3 gather_fusion.1
  23.3 3.2 %all-to-all-start.3 = ((f32[4,1,488]{2,1,0:T(1,128)}), f32[4,1,488]{2,1,0:T(1,128)S(1)}, u32[]{:S(2)}, u32[]{:S(2)}) async-start(f32[4,1,488]{2,1,0:T(1,128)} %reshape.158), calls=%async_computation.3 | async-start | bytes 16384 | tf_op jit(solution)/shard_map/all_to_all | solution.py:68
  27.3 2.7 %gather_fusion.2 = f32[32,61,61]{2,0,1:T(8,128)S(1)} fusion(f32[64,61,61]{2,0,1:T(8,128)S(1)} %copy-done, s32[1024]{0:T(1024)S(1)} %pad_clamp_fusion.1), kind=kCustom, calls=%fused_computation.2 | custom fusion | bytes 952704 | tf_op jit(solution)/shard_map/gather | solution.py:61
  30.0 5.3 %gather_fusion = f32[32,61,61]{2,0,1:T(8,128)} fusion(f32[64,61,61]{2,0,1:T(8,128)} %param.13, s32[1024]{0:T(1024)S(1)} %pad_clamp_fusion.1), kind=kCustom, calls=%fused_computation | custom fusion | bytes 952704 | tf_op jit(solution)/shard_map/gather | solution.py:60
  35.3 3.4 %all-to-all-start.1 = ((f32[4,1,488]{2,1,0:T(1,128)}), f32[4,1,488]{2,1,0:T(1,128)S(1)}, u32[]{:S(2)}, u32[]{:S(2)}) async-start(f32[4,1,488]{2,1,0:T(1,128)} %reshape.160), calls=%async_computation.1 | async-start | bytes 16384 | tf_op jit(solution)/shard_map/all_to_all | solution.py:69
  38.7 2.8 %copy_multiply_fusion.5 = (f32[4,8,61,61]{3,1,2,0:T(8,128)}, f32[4,8,61,61]{3,1,2,0:T(8,128)}) fusion(f32[4,8]{1,0:T(4,128)S(1)} %bitcast_convert_fusion, f32[32,61,61]{2,0,1:T(8,128)S(1)} %gather_fusion.2, f32[32,61,61]{2,0,1:T(8,128)} %gather_fusion), kind=kLoop, calls=%fused_computation.16 | loop fusion | flops 238144 | bytes 1905280 | tf_op jit(solution)/shard_map/mul | solution.py:60
  41.5 3.2 %reshape.162 = f32[4,1,29768]{2,1,0:T(1,128)} reshape(f32[4,61,8,61]{3,2,1,0:T(8,128)} %bitcast.49) | data formatting | bytes 952576
  44.7 3.5 %all-to-all-start = ((f32[4,1,29768]{2,1,0:T(1,128)}), f32[4,1,29768]{2,1,0:T(1,128)S(1)}, u32[]{:S(2)}, u32[]{:S(2)}) async-start(f32[4,1,29768]{2,1,0:T(1,128)} %reshape.162), calls=%async_computation | async-start | bytes 954368 | tf_op jit(solution)/shard_map/all_to_all | solution.py:66
  48.2 3.1 %reshape.156 = f32[4,1,29768]{2,1,0:T(1,128)} reshape(f32[4,61,8,61]{3,2,1,0:T(8,128)} %bitcast.48) | data formatting | bytes 952576
  54.8 1.7 %all-to-all-done = f32[4,1,29768]{2,1,0:T(1,128)S(1)} async-done(((f32[4,1,29768]{2,1,0:T(1,128)}), f32[4,1,29768]{2,1,0:T(1,128)S(1)}, u32[]{:S(2)}, u32[]{:S(2)}) %all-to-all-start) | async-done | bytes 476320 | tf_op jit(solution)/shard_map/all_to_all | solution.py:66
  56.4 4.1 %all-to-all-start.2 = ((f32[4,1,29768]{2,1,0:T(1,128)}), f32[4,1,29768]{2,1,0:T(1,128)}, u32[]{:S(2)}, u32[]{:S(2)}) async-start(f32[4,1,29768]{2,1,0:T(1,128)} %reshape.156), calls=%async_computation.2 | async-start | bytes 954368 | tf_op jit(solution)/shard_map/all_to_all | solution.py:67
  60.9 2.1 %reduce.7 = f32[4,29768]{1,0:T(4,128)S(1)} reduce(f32[4,1,29768]{2,1,0:T(1,128)S(1)} %all-to-all-done, f32[]{:T(128)} %broadcast.86), dimensions={1}, to_apply=%all_to_all.18.reduce_sub_computation | reduce | bytes 952580 | tf_op jit(solution)/shard_map/all_to_all | solution.py:66
  64.3 4.6 %all-to-all-done.2 = f32[4,1,29768]{2,1,0:T(1,128)} async-done(((f32[4,1,29768]{2,1,0:T(1,128)}), f32[4,1,29768]{2,1,0:T(1,128)}, u32[]{:S(2)}, u32[]{:S(2)}) %all-to-all-start.2) | async-done | bytes 476320 | tf_op jit(solution)/shard_map/all_to_all | solution.py:67
  68.9 2.9 %reduce.5 = f32[4,29768]{1,0:T(4,128)S(1)} reduce(f32[4,1,29768]{2,1,0:T(1,128)} %all-to-all-done.2, f32[]{:T(128)} %broadcast.86), dimensions={1}, to_apply=%all_to_all.20.reduce_sub_computation | reduce | bytes 952580 | tf_op jit(solution)/shard_map/all_to_all | solution.py:67
  72.6 6.8 %fusion = f32[8,61,16,128]{3,1,2,0:T(8,128)S(1)} fusion(f32[16,61,8,128]{3,2,1,0:T(8,128)} %bitcast.46, f32[8,61,61,1]{2,0,1,3:T(8,128)S(1)} %bitcast.50), kind=kOutput, calls=%fused_computation.8 | convolution fusion | flops 731578368 | bytes 8114464 | tf_op jit(solution)/shard_map/nkj,bjnl->bknl/dot_general | solution.py:12
  79.5 6.4 %multiply_reduce_fusion.1 = (f32[16,8,128]{2,0,1:T(8,128)S(1)}, f32[16,8,128]{2,0,1:T(8,128)S(1)}, f32[16,8,128]{2,0,1:T(8,128)S(1)}) fusion(f32[61,8]{0,1:T(8,128)S(1)} %copy-done.4, f32[16,61,8]{1,0,2:T(8,128)S(1)} %multiply_exponential_fusion, f32[8,61,16,128]{3,1,2,0:T(8,128)S(1)} %fusion, f32[16,61,8,128]{3,2,1,0:T(8,128)S(1)} %bitcast.61, ...), kind=kOutput, calls=%fused_computation.13 | convolution fusion | flops 739524608 | bytes 8346208 | tf_op jit(solution)/shard_map/binl,nik->bknl/dot_general | solution.py:11
  87.6 53.6 %all-gather.4.cloned.1.call-done = f32[64,16,256]{2,1,0:T(8,128)} async-done(((f32[2,16,256]{2,1,0:T(8,128)}), f32[64,16,256]{2,1,0:T(8,128)}) %all-gather.4.cloned.1.call-update) | async-done | bytes 1048592 | tf_op jit(solution)/shard_map/all_gather | solution.py:85
  141.3 1.3 reduce_sum.118
  142.6 1.4 reduce.2
  (72 shorter events, 11.3 us)
Async XLA Ops:
  7.2 20.1 %copy-start = (f32[64,61,61]{2,0,1:T(8,128)S(1)}, f32[64,61,61]{2,0,1:T(8,128)}, u32[]{:S(2)}) copy-start(f32[64,61,61]{2,0,1:T(8,128)} %param.14) | copy-start | bytes 2857732
  16.4 6.9 %all-to-all-start.4 = ((f32[4,1,8]{2,1,0:T(1,128)}), f32[4,1,8]{2,1,0:T(1,128)S(1)}, u32[]{:S(2)}, u32[]{:S(2)}) async-start(f32[4,1,8]{2,1,0:T(1,128)} %bitcast.14), calls=%async_computation.4 | async-start | bytes 4096 | tf_op jit(solution)/shard_map/all_to_all | solution.py:70
  23.3 12.0 %all-to-all-start.3 = ((f32[4,1,488]{2,1,0:T(1,128)}), f32[4,1,488]{2,1,0:T(1,128)S(1)}, u32[]{:S(2)}, u32[]{:S(2)}) async-start(f32[4,1,488]{2,1,0:T(1,128)} %reshape.158), calls=%async_computation.3 | async-start | bytes 16384 | tf_op jit(solution)/shard_map/all_to_all | solution.py:68
  35.3 12.9 %copy-start.13 = (s32[16]{0:T(128)S(1)}, s32[16]{0:T(128)}, u32[]{:S(2)}) copy-start(s32[16]{0:T(128)} %param.21) | copy-start | bytes 196
  35.3 12.9 %copy-start.7 = (s32[1,1024]{1,0:T(1,128)S(1)}, s32[1,1024]{1,0:T(1,128)}, u32[]{:S(2)}) copy-start(s32[1,1024]{1,0:T(1,128)} %param.19) | copy-start | bytes 12292
  35.3 9.4 %all-to-all-start.1 = ((f32[4,1,488]{2,1,0:T(1,128)}), f32[4,1,488]{2,1,0:T(1,128)S(1)}, u32[]{:S(2)}, u32[]{:S(2)}) async-start(f32[4,1,488]{2,1,0:T(1,128)} %reshape.160), calls=%async_computation.1 | async-start | bytes 16384 | tf_op jit(solution)/shard_map/all_to_all | solution.py:69
  44.7 11.8 %all-to-all-start = ((f32[4,1,29768]{2,1,0:T(1,128)}), f32[4,1,29768]{2,1,0:T(1,128)S(1)}, u32[]{:S(2)}, u32[]{:S(2)}) async-start(f32[4,1,29768]{2,1,0:T(1,128)} %reshape.162), calls=%async_computation | async-start | bytes 954368 | tf_op jit(solution)/shard_map/all_to_all | solution.py:66
  48.2 3.2 %copy-start.9 = (s32[16]{0:T(128)}, s32[16]{0:T(128)S(1)}, u32[]{:S(2)}) copy-start(s32[16]{0:T(128)S(1)} %compare_select_fusion.1) | copy-start | bytes 196
  52.0 8.8 %copy-start.5 = (f32[16]{0:T(128)}, f32[16]{0:T(128)S(1)}, u32[]{:S(2)}) copy-start(f32[16]{0:T(128)S(1)} %gather_fusion.5) | copy-start | bytes 196
  54.8 6.1 %copy-start.3 = (f32[61,8]{0,1:T(8,128)}, f32[61,8]{0,1:T(8,128)S(1)}, u32[]{:S(2)}) copy-start(f32[61,8]{0,1:T(8,128)S(1)} %multiply_bitcast_fusion) | copy-start | bytes 5860
  56.4 12.5 %all-to-all-start.2 = ((f32[4,1,29768]{2,1,0:T(1,128)}), f32[4,1,29768]{2,1,0:T(1,128)}, u32[]{:S(2)}, u32[]{:S(2)}) async-start(f32[4,1,29768]{2,1,0:T(1,128)} %reshape.156), calls=%async_computation.2 | async-start | bytes 954368 | tf_op jit(solution)/shard_map/all_to_all | solution.py:67
  60.6 80.7 %all-gather.4.cloned.1.call-start = ((), (), s32[]{:S(2)}) async-start(), calls=%async_computation.5 | async-start | bytes 1081344 | tf_op jit(solution)/shard_map/all_gather | solution.py:85
  72.5 6.9 %copy-start.2 = (f32[8,61,61]{2,0,1:T(8,128)S(1)}, f32[8,61,61]{2,0,1:T(8,128)}, u32[]{:S(2)}) copy-start(f32[8,61,61]{2,0,1:T(8,128)} %bitcast_reduce_fusion) | copy-start | bytes 357220
  72.5 6.9 %copy-start.4 = (f32[61,8]{0,1:T(8,128)S(1)}, f32[61,8]{0,1:T(8,128)}, u32[]{:S(2)}) copy-start(f32[61,8]{0,1:T(8,128)} %copy-done.3) | copy-start | bytes 5860
  72.5 6.9 %copy-start.8 = (f32[8,61]{1,0:T(8,128)S(1)}, f32[8,61]{1,0:T(8,128)}, u32[]{:S(2)}) copy-start(f32[8,61]{1,0:T(8,128)} %reduce_sum.109) | copy-start | bytes 5860
  72.5 6.9 %copy-start.12 = (f32[16,61,1,1024]{3,2,1,0:T(1,128)S(1)}, f32[16,61,1,1024]{3,2,1,0:T(1,128)}, u32[]{:S(2)}) copy-start(f32[16,61,1,1024]{3,2,1,0:T(1,128)} %param.11) | copy-start | bytes 11993092
  79.4 6.6 %copy-start.11 = (s32[1,8]{1,0:T(1,128)S(1)}, s32[1,8]{1,0:T(1,128)}, u32[]{:S(2)}) copy-start(s32[1,8]{1,0:T(1,128)} %param.20) | copy-start | bytes 100
  79.4 64.6 %copy-start.6 = (f32[16]{0:T(128)S(1)}, f32[16]{0:T(128)}, u32[]{:S(2)}) copy-start(f32[16]{0:T(128)} %copy-done.5) | copy-start | bytes 196
  79.4 64.6 %copy-start.10 = (s32[16]{0:T(128)S(1)}, s32[16]{0:T(128)}, u32[]{:S(2)}) copy-start(s32[16]{0:T(128)} %copy-done.9) | copy-start | bytes 196
  144.7 0.7 copy-start.1
Sparse Core Ops, SparseCore 0:
  87.0 54.2 all-gather.3
